TPU v7x, 512 devices: a whole 4x8x8 slice. The times are simulated.
512 devices in a mesh: row: 16 (over y, core), col: 32 (over z, x).
Axes of the slice: x: 4, y: 8, z: 8, core: 2. Of those that a mesh axis runs over, the one named last changes fastest.
Arguments:
- offsets: float32 [3, 131072], P(None, ('row', 'col')), may hold values from 0 to 11
- cells: int32 [3, 1024], replicated, may hold values from 0 to 15, as said below
- types: int32 [131072], P(('row', 'col')), may hold values from 0 to 3, as said below
- mask: int32 [16, 64, 16, 64], P(None, 'col', 'row'), may hold values from 0 to 1, as said below
- chi_table: float32 [4], replicated, may hold values from 2 to 10.1
- eta_table: float32 [4], replicated, may hold values from 13 to 18
- gamma_table: float32 [4], replicated, may hold values from 0.4 to 0.8
Outputs:
- charges: float32 [131072], P(('row', 'col'))
Inputs may be any that keep to these rules, and one draw needn't show every extreme that they name: The cells of the blocks are a permutation of all 16 x 16 x 4 cells: each cell holds exactly one block. The mask marks a pair of blocks exactly when their cells are equal or adjacent on the periodic grid in every dimension; it is symmetric and each block is marked with exactly 27 blocks, itself included. `types`: types 2 and 3 grow more common along the atoms, from none in the first 256 atoms to nearly all in the last.
All inputs are finite; a program needn't handle non-finite values.
Results may differ from a plain program's by a relative error of at most 0.0003.
Values sent between devices are 32-bit elements; how exact they have to be, the bound alone decides.
A program may use at most 64 MiB of HBM per device.

v0:
```python
import jax
import jax.numpy as jnp
from jax import lax
from jax.sharding import Mesh
from jax.sharding import PartitionSpec as P

BLOCK = 128
GRID_Z = 4
ITERS = 3
ROW_COL = ("row_0", "row_1", "col_0", "col_1")
ROW = ("row_0", "row_1")
COL = ("col_0", "col_1")
coulomb = 14.4
cutoff = 10.0
cell_side = 11.0
pair_group = 64


def copy_for_each(value, axis):
    devices = lax.axis_size(axis)
    return lax.all_to_all(
        jnp.broadcast_to(value[None], (devices, *value.shape)), axis, 0, 0, tiled=True
    )


def over_copies(value, axis):
    return copy_for_each(value, axis).sum(axis=0)


def over_axes(value, axes):
    far, near = axes
    return over_copies(over_copies(value, near), far)


def in_one(arrays, axis):
    line, at, outs = (jnp.concatenate([a.reshape(-1) for a in arrays]), 0, [])
    subtotal = over_axes(line, axis)
    for a in arrays:
        outs.append(subtotal[at : at + a.size].reshape(a.shape))
        at += a.size
    return tuple(outs)


def in_order(blocks, dim):
    blocks = jnp.moveaxis(blocks, 0, dim)
    lengths = blocks.shape
    return blocks.reshape(*lengths[:dim], lengths[dim] * lengths[dim + 1], *lengths[dim + 2 :])


def gathered_copies(value, axis, dim):
    return in_order(copy_for_each(value, axis), dim)


def in_blocks(value, dim, devices):
    before, after = (value.shape[:dim], value.shape[dim + 1 :])
    return jnp.moveaxis(value.reshape(*before, devices, -1, *after), dim, 0)


def sent_and_summed(value, axis, dim):
    devices = lax.axis_size(axis)
    blocks = lax.all_to_all(in_blocks(value, dim, devices), axis, 0, 0, tiled=True)
    return jnp.sum(blocks, axis=0)


def taper(dist):
    xval = dist / cutoff
    poly = 1.0 + xval**4 * (-35.0 + xval * (84.0 + xval * (-70.0 + 20.0 * xval)))
    return jnp.where(xval < 1.0, poly, 0.0)


def coupling(tgt, src, tgt_cell, src_cell, same, grid):
    half = grid[:, None] // 2
    shift = ((src_cell - tgt_cell + half) % grid[:, None] - half).astype(jnp.float32) * cell_side
    radius_sq = jnp.zeros((tgt.shape[1], tgt.shape[2], src.shape[2]), jnp.float32)
    for comp in range(3):
        delta = shift[comp][:, None, None] + src[comp][:, None, :] - tgt[comp][:, :, None]
        radius_sq = radius_sq + delta * delta
    dist = jnp.sqrt(radius_sq)
    paired = tgt[3][:, :, None] * src[3][:, None, :]
    shield = 1.0 / (paired * jnp.sqrt(paired))
    kern = coulomb * taper(dist) / jnp.cbrt(radius_sq * dist + shield)
    width = tgt.shape[2]
    diag = jnp.arange(width)[:, None] == jnp.arange(width)[None, :]
    return jnp.where(same[:, None, None] & diag[None], 0.0, kern)


def pick(kinds, table):
    return jnp.sum(jnp.where(kinds, table[:, None], 0.0), axis=0)


def paired_sums(residual, image):
    return in_one(
        (jnp.sum(residual * residual, axis=1), jnp.sum(residual * image, axis=1)),
        ("row_0", ("row_1", "col_0", "col_1")),
    )


def per_device(offsets, cells, types, mask, chi_table, eta_table, gamma_table):
    n_row = lax.axis_size(ROW)
    n_col = lax.axis_size(COL)
    row_at = lax.axis_index(ROW)
    col_at = lax.axis_index(COL)
    span = types.shape[0]
    bpd = span // BLOCK
    n_tgt = n_row * bpd
    n_src = n_col * bpd
    grid = jnp.array([n_row, n_src // GRID_Z, GRID_Z], jnp.int32)
    kinds = jnp.arange(chi_table.shape[0])[:, None] == types[None, :]
    chi = pick(kinds, chi_table)
    eta = pick(kinds, eta_table)
    gamma = pick(kinds, gamma_table)
    geo = jnp.concatenate([offsets, gamma[None]], axis=0)
    src_geo = gathered_copies(geo, COL, 1).reshape(4, n_src, BLOCK)
    tgt_geo = lax.all_gather(geo, ROW, axis=1, tiled=True).reshape(4, n_tgt, BLOCK)
    tgt_ids = (
        (jnp.arange(n_row, dtype=jnp.int32)[:, None] * n_col + col_at) * bpd
        + jnp.arange(bpd, dtype=jnp.int32)[None, :]
    ).reshape(n_tgt)
    src_ids = row_at * n_src + jnp.arange(n_src, dtype=jnp.int32)
    tgt_cells = jnp.take(cells, tgt_ids, axis=1)
    src_cells = jnp.take(cells, src_ids, axis=1)
    tile = mask.reshape(n_tgt * n_src)
    count = jnp.sum(tile)
    slots = jnp.nonzero(tile, size=n_tgt * n_src + pair_group, fill_value=0)[0].astype(jnp.int32)
    groups = (count + pair_group - 1) // pair_group
    src_range = jnp.arange(n_src, dtype=jnp.int32)

    def block_kernel(step):
        picked = lax.dynamic_slice_in_dim(slots, step * pair_group, pair_group)
        live = step * pair_group + jnp.arange(pair_group) < count
        tgt_blk = picked // n_src
        src_blk = picked % n_src
        kern = coupling(
            tgt_geo[:, tgt_blk],
            src_geo[:, src_blk],
            tgt_cells[:, tgt_blk],
            src_cells[:, src_blk],
            tgt_ids[tgt_blk] == src_ids[src_blk],
            grid,
        )
        return (jnp.where(live[:, None, None], kern, 0.0), tgt_blk, src_blk)

    def apply(direction):
        remote = lax.all_gather(direction, ROW, axis=1, tiled=True).reshape(2, n_tgt, BLOCK)

        def turn(step, acc):
            kern, tgt_blk, src_blk = block_kernel(step)
            contrib = jnp.einsum(
                "gij,kgi->kgj", kern, remote[:, tgt_blk], precision=lax.Precision.HIGHEST
            )
            owners = (src_range[:, None] == src_blk[None, :]).astype(jnp.float32)
            return acc + jnp.einsum("sg,kgj->ksj", owners, contrib, precision=lax.Precision.HIGHEST)

        acc = lax.fori_loop(0, groups, turn, jnp.zeros((2, n_src, BLOCK), jnp.float32))
        summed = sent_and_summed(acc.reshape(2, n_src * BLOCK), COL, 1)
        return summed + eta[None] * direction

    rhs = jnp.stack([-chi, -jnp.ones_like(chi)], axis=0)
    solution = jnp.zeros_like(rhs)
    residual = rhs
    image = apply(residual)
    norm_now, product = paired_sums(residual, image)
    alpha = norm_now / product
    direction = residual
    along = image
    for step in range(ITERS):
        solution = solution + alpha[:, None] * direction
        residual = residual - alpha[:, None] * along
        if step + 1 < ITERS:
            image = apply(residual)
            norm_next, product = paired_sums(residual, image)
            ratio = norm_next / norm_now
            alpha = norm_next / (product - ratio * norm_next / alpha)
            direction = residual + ratio[:, None] * direction
            along = image + ratio[:, None] * along
            norm_now = norm_next
    totals = over_axes(jnp.sum(solution, axis=1), ("row_0", ("row_1", "col_0", "col_1")))
    return solution[0] - totals[0] / totals[1] * solution[1]


def solution(mesh):
    torus = Mesh(mesh.devices.reshape(8, 2, 8, 4), ("row_0", "row_1", "col_0", "col_1"))
    placed = (P(None, ROW_COL), P(), P(ROW_COL), P(None, COL, ROW, None), P(), P(), P())
    return jax.shard_map(
        per_device, mesh=torus, in_specs=placed, out_specs=P(ROW_COL), check_vma=False
    )
```

profile of v0, /device:TPU:1, one launch (start us, length us, event | category | flops | bytes accessed | tf_op | source)
XLA Modules:
  0.0 372.8 jit_solution(4462579200094896409)
XLA Ops:
  0.0 0.8 select_reduce_fusion
  2.2 13.7 %all-to-all-start = ((f32[32,4,256]{2,1,0:T(4,128)}), f32[32,4,256]{2,1,0:T(4,128)S(1)}, u32[]{:S(2)}, u32[]{:S(2)}) async-start(f32[32,4,256]{2,1,0:T(4,128)} %broadcast_in_dim.293), calls=%async_computation | async-start | bytes 262144 | tf_op jit(solution)/shard_map/all_to_all | solution.py:21
  15.9 1.4 fusion.201
  20.4 14.7 %scatter_custom_fusion = s32[2112]{0:T(1024)S(1)} fusion(s32[2048]{0:T(1024)S(1)} %bitcast.241, s32[2048]{0:T(1024)S(1)} %broadcast.958, s32[]{:T(128)} %constant.520.clone.1), kind=kCustom, calls=%fused_computation.302 | custom fusion | flops 2048 | bytes 8452 | tf_op jit(solution)/shard_map/scatter-add | solution.py:124
  35.7 18.5 %all_gather.12 = f32[2,4096]{1,0:T(2,128)S(1)} all-gather(f32[2,256]{1,0:T(2,128)S(1)} %stack.2), channel_id=1, replica_groups=mesh['row_0'=8,'row_1'=2,'col_0'=8,'col_1'=4] {'row_0','row_1'}, dimensions={1}, use_global_device_ids=true | all-gather | bytes 34816 | tf_op jit(solution)/shard_map/all_gather | solution.py:144
  54.9 15.1 %all_gather.13 = f32[4,4096]{1,0:T(4,128)S(1)} all-gather(f32[4,256]{1,0:T(4,128)S(1)} %pad_maximum_fusion), channel_id=1, replica_groups=mesh['row_0'=8,'row_1'=2,'col_0'=8,'col_1'=4] {'row_0','row_1'}, dimensions={1}, use_global_device_ids=true | all-gather | bytes 69632 | tf_op jit(solution)/shard_map/all_gather | solution.py:114
  70.1 21.0 %while.48 = (s32[]{:T(128)}, f32[2,64,128]{2,1,0:T(8,128)S(1)}, s32[]{:T(128)}, s32[2112]{0:T(1024)S(1)}, f32[2,32,128]{2,0,1:T(2,128)S(1)}, /*index=5*/s32[]{:T...) while((s32[]{:T(128)}, f32[2,64,128]{2,1,0:T(8,128)S(1)}, ...), condition=%wide.region_11.13_spmd.clone.clone.clone, body=%wide.region_10.12_spmd.sunk.clone.clone.clone.sunk | while | flops 70322144 | bytes 2021583 | solution.py:154
  73.0 0.8 gather_fusion.5
  74.0 0.8 gather_fusion.4
  76.8 14.2 %fusion.249 = f32[2,64,128]{2,0,1:T(2,128)S(1)} fusion(f32[64,128]{1,0:T(8,128)S(1)} %bitcast.216, f32[64,128]{1,0:T(8,128)S(1)} %bitcast.222, f32[64,128]{1,0:T(8,128)S(1)} %bitcast.220, f32[64,128]{1,0:T(8,128)S(1)} %broadcast_add_fusion.19, f32[64,128]{1,0:T(8,128)S(1)} %bitcast.221, f32[64,128]{1,0:T(8,128)S(1)} %broadcast_add_fusion.20, ...), kind=kOutput, calls=%fused_computation.77.clone.1 | convolution fusion | flops 57671680 | bytes 409728 | tf_op jit(solution)/shard_map/while/body/gij,kgi->kgj/dot_general | solution.py:148
  91.3 18.1 %all_to_all.68 = f32[32,2,256]{2,1,0:T(2,128)S(1)} all-to-all(f32[32,2,256]{2,1,0:T(2,128)S(1)} %copy.39), channel_id=1, replica_groups=mesh['row_0'=8,'row_1'=2,'col_0'=8,'col_1'=4] {'col_0','col_1'}, dimensions={0} | all-to-all | bytes 131072 | tf_op jit(solution)/shard_map/all_to_all | solution.py:61
  109.7 14.1 %all_to_all.69 = f32[64,1,4]{2,1,0:T(1,128)S(1)} all-to-all(f32[64,1,4]{2,1,0:T(1,128)S(1)} %broadcast_in_dim.295), channel_id=1, replica_groups=mesh['row_0'=8,'row_1'=2,'col_0'=8,'col_1'=4] {'row_1','col_0','col_1'}, dimensions={0} | all-to-all | bytes 2048 | tf_op jit(solution)/shard_map/all_to_all | solution.py:21
  124.5 24.5 %all-to-all-start.3 = ((f32[8,1,4]{2,1,0:T(1,128)}), f32[8,1,4]{2,1,0:T(1,128)S(1)}, u32[]{:S(2)}, u32[]{:S(2)}) async-start(f32[8,1,4]{2,1,0:T(1,128)} %broadcast_in_dim.296), calls=%async_computation.3 | async-start | bytes 8192 | tf_op jit(solution)/shard_map/all_to_all | solution.py:21
  149.1 6.6 %all-to-all-done.3 = f32[8,1,4]{2,1,0:T(1,128)S(1)} async-done(((f32[8,1,4]{2,1,0:T(1,128)}), f32[8,1,4]{2,1,0:T(1,128)S(1)}, u32[]{:S(2)}, u32[]{:S(2)}) %all-to-all-start.3) | async-done | bytes 160 | tf_op jit(solution)/shard_map/all_to_all | solution.py:21
  155.8 16.5 %all_gather.14 = f32[2,4096]{1,0:T(2,128)S(1)} all-gather(f32[2,256]{1,0:T(2,128)S(1)} %multiply_subtract_fusion.1), channel_id=1, replica_groups=mesh['row_0'=8,'row_1'=2,'col_0'=8,'col_1'=4] {'row_0','row_1'}, dimensions={1}, use_global_device_ids=true | all-gather | bytes 34816 | tf_op jit(solution)/shard_map/all_gather | solution.py:144
  172.4 21.0 %while.49 = (s32[]{:T(128)}, f32[2,64,128]{2,1,0:T(8,128)S(1)}, s32[]{:T(128)}, s32[2112]{0:T(1024)S(1)}, f32[2,32,128]{2,0,1:T(2,128)S(1)}, /*index=5*/s32[]{:T...) while((s32[]{:T(128)}, f32[2,64,128]{2,1,0:T(8,128)S(1)}, ...), condition=%wide.region_19.21_spmd.clone.clone.clone, body=%wide.region_18.20_spmd.sunk.clone.clone.clone.sunk | while | flops 70322144 | bytes 2021583 | solution.py:154
  175.2 0.8 gather_fusion.12
  176.2 0.8 gather_fusion.11
  179.0 14.2 %fusion.258 = f32[2,64,128]{2,0,1:T(2,128)S(1)} fusion(f32[64,128]{1,0:T(8,128)S(1)} %bitcast.217, f32[64,128]{1,0:T(8,128)S(1)} %bitcast.226, f32[64,128]{1,0:T(8,128)S(1)} %bitcast.224, f32[64,128]{1,0:T(8,128)S(1)} %broadcast_add_fusion.22, f32[64,128]{1,0:T(8,128)S(1)} %bitcast.225, f32[64,128]{1,0:T(8,128)S(1)} %broadcast_add_fusion.23, ...), kind=kOutput, calls=%fused_computation.161.clone.1 | convolution fusion | flops 57671680 | bytes 409728 | tf_op jit(solution)/shard_map/while/body/gij,kgi->kgj/dot_general | solution.py:148
  193.5 11.8 %all_to_all.70 = f32[32,2,256]{2,1,0:T(2,128)S(1)} all-to-all(f32[32,2,256]{2,1,0:T(2,128)S(1)} %copy.42), channel_id=1, replica_groups=mesh['row_0'=8,'row_1'=2,'col_0'=8,'col_1'=4] {'col_0','col_1'}, dimensions={0} | all-to-all | bytes 131072 | tf_op jit(solution)/shard_map/all_to_all | solution.py:61
  205.7 14.0 %all_to_all.71 = f32[64,1,4]{2,1,0:T(1,128)S(1)} all-to-all(f32[64,1,4]{2,1,0:T(1,128)S(1)} %broadcast_in_dim.297), channel_id=1, replica_groups=mesh['row_0'=8,'row_1'=2,'col_0'=8,'col_1'=4] {'row_1','col_0','col_1'}, dimensions={0} | all-to-all | bytes 2048 | tf_op jit(solution)/shard_map/all_to_all | solution.py:21
  220.3 24.5 %all-to-all-start.6 = ((f32[8,1,4]{2,1,0:T(1,128)}), f32[8,1,4]{2,1,0:T(1,128)S(1)}, u32[]{:S(2)}, u32[]{:S(2)}) async-start(f32[8,1,4]{2,1,0:T(1,128)} %broadcast_in_dim.298), calls=%async_computation.6 | async-start | bytes 8192 | tf_op jit(solution)/shard_map/all_to_all | solution.py:21
  244.8 6.6 %all-to-all-done.6 = f32[8,1,4]{2,1,0:T(1,128)S(1)} async-done(((f32[8,1,4]{2,1,0:T(1,128)}), f32[8,1,4]{2,1,0:T(1,128)S(1)}, u32[]{:S(2)}, u32[]{:S(2)}) %all-to-all-start.6) | async-done | bytes 160 | tf_op jit(solution)/shard_map/all_to_all | solution.py:21
  251.6 16.5 %all_gather.15 = f32[2,4096]{1,0:T(2,128)S(1)} all-gather(f32[2,256]{1,0:T(2,128)S(1)} %multiply_subtract_fusion), channel_id=1, replica_groups=mesh['row_0'=8,'row_1'=2,'col_0'=8,'col_1'=4] {'row_0','row_1'}, dimensions={1}, use_global_device_ids=true | all-gather | bytes 34816 | tf_op jit(solution)/shard_map/all_gather | solution.py:144
  268.1 21.0 %while.50 = (s32[]{:T(128)}, f32[2,64,128]{2,1,0:T(8,128)S(1)}, s32[]{:T(128)}, s32[2112]{0:T(1024)S(1)}, f32[2,32,128]{2,0,1:T(2,128)S(1)}, /*index=5*/s32[]{:T...) while((s32[]{:T(128)}, f32[2,64,128]{2,1,0:T(8,128)S(1)}, ...), condition=%wide.region_26.28_spmd.clone.clone.clone, body=%wide.region_25.27_spmd.sunk.clone.clone.clone.sunk | while | flops 70322144 | bytes 2021583 | solution.py:154
  271.0 0.8 gather_fusion.19
  274.7 14.2 %fusion.267 = f32[2,64,128]{2,0,1:T(2,128)S(1)} fusion(f32[64,128]{1,0:T(8,128)S(1)} %bitcast.218, f32[64,128]{1,0:T(8,128)S(1)} %bitcast.230, f32[64,128]{1,0:T(8,128)S(1)} %bitcast.228, f32[64,128]{1,0:T(8,128)S(1)} %broadcast_add_fusion.25, f32[64,128]{1,0:T(8,128)S(1)} %bitcast.229, f32[64,128]{1,0:T(8,128)S(1)} %broadcast_add_fusion.26, ...), kind=kOutput, calls=%fused_computation.245.clone.1 | convolution fusion | flops 57671680 | bytes 409728 | tf_op jit(solution)/shard_map/while/body/gij,kgi->kgj/dot_general | solution.py:148
  289.2 11.8 %all_to_all.72 = f32[32,2,256]{2,1,0:T(2,128)S(1)} all-to-all(f32[32,2,256]{2,1,0:T(2,128)S(1)} %copy.45), channel_id=1, replica_groups=mesh['row_0'=8,'row_1'=2,'col_0'=8,'col_1'=4] {'col_0','col_1'}, dimensions={0} | all-to-all | bytes 131072 | tf_op jit(solution)/shard_map/all_to_all | solution.py:61
  301.4 14.0 %all_to_all.73 = f32[64,1,4]{2,1,0:T(1,128)S(1)} all-to-all(f32[64,1,4]{2,1,0:T(1,128)S(1)} %broadcast_in_dim.299), channel_id=1, replica_groups=mesh['row_0'=8,'row_1'=2,'col_0'=8,'col_1'=4] {'row_1','col_0','col_1'}, dimensions={0} | all-to-all | bytes 2048 | tf_op jit(solution)/shard_map/all_to_all | solution.py:21
  315.5 30.9 %all_to_all.74 = f32[8,1,4]{2,1,0:T(1,128)S(1)} all-to-all(f32[8,1,4]{2,1,0:T(1,128)S(1)} %broadcast_in_dim.300), channel_id=1, replica_groups=mesh['row_0'=8,'row_1'=2,'col_0'=8,'col_1'=4] {'row_0'}, dimensions={0} | all-to-all | bytes 256 | tf_op jit(solution)/shard_map/all_to_all | solution.py:21
  346.7 14.5 %all_to_all.75 = f32[64,1,2]{2,1,0:T(1,128)S(1)} all-to-all(f32[64,1,2]{2,1,0:T(1,128)S(1)} %broadcast_in_dim.301), channel_id=1, replica_groups=mesh['row_0'=8,'row_1'=2,'col_0'=8,'col_1'=4] {'row_1','col_0','col_1'}, dimensions={0} | all-to-all | bytes 1024 | tf_op jit(solution)/shard_map/all_to_all | solution.py:21
  361.3 8.9 %all_to_all.76 = f32[8,1,2]{2,1,0:T(1,128)S(1)} all-to-all(f32[8,1,2]{2,1,0:T(1,128)S(1)} %broadcast_in_dim.302), channel_id=1, replica_groups=mesh['row_0'=8,'row_1'=2,'col_0'=8,'col_1'=4] {'row_0'}, dimensions={0} | all-to-all | bytes 128 | tf_op jit(solution)/shard_map/all_to_all | solution.py:21
  (152 shorter events, 26.0 us)
Async XLA Ops:
  0.0 18.2 %copy-start.3 = (s32[3,1024]{1,0:T(4,128)S(1)}, s32[3,1024]{1,0:T(4,128)}, u32[]{:S(2)}) copy-start(s32[3,1024]{1,0:T(4,128)} %param.17) | copy-start | bytes 36868
  2.2 67.9 %all-to-all-start = ((f32[32,4,256]{2,1,0:T(4,128)}), f32[32,4,256]{2,1,0:T(4,128)S(1)}, u32[]{:S(2)}, u32[]{:S(2)}) async-start(f32[32,4,256]{2,1,0:T(4,128)} %broadcast_in_dim.293), calls=%async_computation | async-start | bytes 262144 | tf_op jit(solution)/shard_map/all_to_all | solution.py:21
  18.2 51.9 %copy-start = (s32[3]{0:T(128)S(1)}, s32[3]{0:T(128)}, u32[]{:S(2)}) copy-start(s32[3]{0:T(128)} %constant.962) | copy-start | bytes 40
  18.2 51.9 %copy-start.1 = (s32[3]{0:T(128)S(1)}, s32[3]{0:T(128)}, u32[]{:S(2)}) copy-start(s32[3]{0:T(128)} %constant.963) | copy-start | bytes 40
  18.2 51.9 %copy-start.2 = (s32[3]{0:T(128)S(1)}, s32[3]{0:T(128)}, u32[]{:S(2)}) copy-start(s32[3]{0:T(128)} %constant.964) | copy-start | bytes 40
  124.5 31.1 %all-to-all-start.3 = ((f32[8,1,4]{2,1,0:T(1,128)}), f32[8,1,4]{2,1,0:T(1,128)S(1)}, u32[]{:S(2)}, u32[]{:S(2)}) async-start(f32[8,1,4]{2,1,0:T(1,128)} %broadcast_in_dim.296), calls=%async_computation.3 | async-start | bytes 8192 | tf_op jit(solution)/shard_map/all_to_all | solution.py:21
  220.3 31.1 %all-to-all-start.6 = ((f32[8,1,4]{2,1,0:T(1,128)}), f32[8,1,4]{2,1,0:T(1,128)S(1)}, u32[]{:S(2)}, u32[]{:S(2)}) async-start(f32[8,1,4]{2,1,0:T(1,128)} %broadcast_in_dim.298), calls=%async_computation.6 | async-start | bytes 8192 | tf_op jit(solution)/shard_map/all_to_all | solution.py:21
where the time goes:
time: 374 us; the launch traced here: 373 us
  blocking collectives  205 us (55%)
  starting transfers between devices  62.8 us (17%)
  matrix products  43.2 us (12%)
  other arithmetic  25.8 us (7%)
  local copies, waits for them, and re-layouts  20.5 us (5%)
  waiting for transfers between devices  13.1 us (4%)
    all_to_all x6, blocking collectives, copy_for_each(): lax.all_to_all(jnp.broadcast_to(value[None], (devices, *value.shape)), ax...  96.4 us
    all_to_all x3, starting transfers between devices, copy_for_each(): lax.all_to_all(jnp.broadcast_to(value[None], (devices, *value.shape)), ax...  62.8 us
    all_gather x3, blocking collectives, apply(): lax.all_gather(direction, ROW, axis=1, tiled=True).reshape(2, n_tgt, BLOCK)  51.5 us
    dot_general x3, matrix products, turn(): jnp.einsum('gij,kgi->kgj', kern, remote[:, tgt_blk], precision=lax.Precis...  42.6 us
    all_to_all x3, blocking collectives, sent_and_summed(): lax.all_to_all(in_blocks(value, dim, devices), axis, 0, 0, tiled=True)  41.8 us
    all_gather x1, blocking collectives, per_device(): lax.all_gather(geo, ROW, axis=1, tiled=True).reshape(4, n_tgt, BLOCK)  15.1 us
    scatter-add x1, other arithmetic, per_device(): jnp.nonzero(tile, size=n_tgt * n_src + pair_group, fill_value=0)[0]  14.7 us
    all_to_all x3, waiting for transfers between devices, copy_for_each(): lax.all_to_all(jnp.broadcast_to(value[None], (devices, *value.shape)), ax...  13.1 us
  transfers between devices with their start and end apart: 3, of which 2 were waited for; matrix products, arithmetic and copies ran while one was open for 5% of the time, Pallas kernels for 0%

commit v1 on v0

--- a/solution.py
+++ b/solution.py
@@ -14,6 +14,14 @@
 cutoff = 10.0
 cell_side = 11.0
 pair_group = 64
+
+
+def cut_lines(frame_in, axis_id, dimension_no):
+    z2 = jnp.concatenate(
+        jax.lax.all_to_all(jnp.stack([frame_in] * jax.lax.axis_size(axis_id)), axis_id, 0, 0),
+        axis=dimension_no,
+    )
+    return z2
 
 
 def copy_for_each(value, axis):
@@ -141,7 +149,7 @@
         return (jnp.where(live[:, None, None], kern, 0.0), tgt_blk, src_blk)
 
     def apply(direction):
-        remote = lax.all_gather(direction, ROW, axis=1, tiled=True).reshape(2, n_tgt, BLOCK)
+        remote = cut_lines(direction, ROW, 1).reshape(2, n_tgt, BLOCK)
 
         def turn(step, acc):
             kern, tgt_blk, src_blk = block_kernel(step)

time: 374 us -> 355 us (0.949)
  starting transfers between devices: 62.8 us -> 32 us
  blocking collectives: 205 us -> 215 us
    all_to_all x6 -> x8, blocking collectives: 96.4 us -> 155 us  [copy_for_each(): lax.all_to_all(jnp.broadcast_to(value[None], (devices, *value.shape)), ax...]
    all_gather x3 -> x0, blocking collectives: 51.5 us -> none  [apply(): lax.all_gather(direction, ROW, axis=1, tiled=True).reshape(2, n_tgt, BLOCK)]
    all_to_all x3 -> x1, starting transfers between devices: 62.8 us -> 11.4 us  [copy_for_each(): lax.all_to_all(jnp.broadcast_to(value[None], (devices, *value.shape)), ax...]
    all_to_all x0 -> x3, starting transfers between devices: none -> 20.6 us  [cut_lines(): jax.lax.all_to_all(jnp.stack([frame_in] * jax.lax.axis_size(axis_id)), ax...]
    all_to_all x0 -> x3, waiting for transfers between devices: none -> 15 us  [cut_lines(): jax.lax.all_to_all(jnp.stack([frame_in] * jax.lax.axis_size(axis_id)), ax...]
    all_to_all x3 -> x1, waiting for transfers between devices: 13.1 us -> 0.01 us  [copy_for_each(): lax.all_to_all(jnp.broadcast_to(value[None], (devices, *value.shape)), ax...]
  transfers between devices with their start and end apart: 3 -> 4, of which waited for: 2 -> 2; matrix products, arithmetic and copies ran while one was open for 5% -> 6% of each run, Pallas kernels for 0% -> 0%
where the time goes in v1:
time: 355 us; the launch traced here: 354 us
  blocking collectives  215 us (61%)
  matrix products  43.2 us (12%)
  starting transfers between devices  32 us (9%)
  other arithmetic  25.1 us (7%)
  local copies, waits for them, and re-layouts  21.8 us (6%)
  waiting for transfers between devices  15 us (4%)
    all_to_all x8, blocking collectives, copy_for_each(): lax.all_to_all(jnp.broadcast_to(value[None], (devices, *value.shape)), ax...  155 us
    dot_general x3, matrix products, turn(): jnp.einsum('gij,kgi->kgj', kern, remote[:, tgt_blk], precision=lax.Precis...  42.6 us
    all_to_all x3, blocking collectives, sent_and_summed(): lax.all_to_all(in_blocks(value, dim, devices), axis, 0, 0, tiled=True)  41.8 us
    all_to_all x3, starting transfers between devices, cut_lines(): jax.lax.all_to_all(jnp.stack([frame_in] * jax.lax.axis_size(axis_id)), ax...  20.6 us
    all_gather x1, blocking collectives, per_device(): lax.all_gather(geo, ROW, axis=1, tiled=True).reshape(4, n_tgt, BLOCK)  17.6 us
    all_to_all x3, waiting for transfers between devices, cut_lines(): jax.lax.all_to_all(jnp.stack([frame_in] * jax.lax.axis_size(axis_id)), ax...  15 us
    scatter-add x1, other arithmetic, per_device(): jnp.nonzero(tile, size=n_tgt * n_src + pair_group, fill_value=0)[0]  14.7 us
    all_to_all x1, starting transfers between devices, copy_for_each(): lax.all_to_all(jnp.broadcast_to(value[None], (devices, *value.shape)), ax...  11.4 us
  transfers between devices with their start and end apart: 4, of which 2 were waited for; matrix products, arithmetic and copies ran while one was open for 6% of the time, Pallas kernels for 0%

profile of v1, /device:TPU:1, one launch (start us, length us, event | category | flops | bytes accessed | tf_op | source)
XLA Modules:
  0.0 354.4 jit_solution(1485966386819533454)
XLA Ops:
  0.0 0.8 select_reduce_fusion
  1.4 10.1 %all-to-all-start = ((f32[16,2,256]{2,1,0:T(2,128)}), f32[16,2,256]{2,1,0:T(2,128)S(1)}, u32[]{:S(2)}, u32[]{:S(2)}) async-start(f32[16,2,256]{2,1,0:T(2,128)} %stack.9), calls=%async_computation | async-start | bytes 65536 | tf_op jit(solution)/shard_map/all_to_all | solution.py:21
  11.5 1.4 fusion.201
  13.9 0.9 copy.37
  16.8 14.7 %scatter_custom_fusion = s32[2112]{0:T(1024)S(1)} fusion(s32[2048]{0:T(1024)S(1)} %bitcast.247, s32[2048]{0:T(1024)S(1)} %broadcast.964, s32[]{:T(128)} %constant.520.clone.1), kind=kCustom, calls=%fused_computation.302 | custom fusion | flops 2048 | bytes 8452 | tf_op jit(solution)/shard_map/scatter-add | solution.py:132
  33.5 11.4 %all-to-all-start.1 = ((f32[32,4,256]{2,1,0:T(4,128)}), f32[32,4,256]{2,1,0:T(4,128)S(1)}, u32[]{:S(2)}, u32[]{:S(2)}) async-start(f32[32,4,256]{2,1,0:T(4,128)} %broadcast_in_dim.293), calls=%async_computation.1 | async-start | bytes 262144 | tf_op jit(solution)/shard_map/all_to_all | solution.py:29
  44.9 17.6 %all_gather.3 = f32[4,4096]{1,0:T(4,128)S(1)} all-gather(f32[4,256]{1,0:T(4,128)S(1)} %pad_maximum_fusion), channel_id=1, replica_groups=mesh['row_0'=8,'row_1'=2,'col_0'=8,'col_1'=4] {'row_0','row_1'}, dimensions={1}, use_global_device_ids=true | all-gather | bytes 69632 | tf_op jit(solution)/shard_map/all_gather | solution.py:122
  62.7 21.0 %while.48 = (s32[]{:T(128)}, f32[2,64,128]{2,1,0:T(8,128)S(1)}, s32[]{:T(128)}, s32[2112]{0:T(1024)S(1)}, f32[2,32,128]{2,0,1:T(2,128)S(1)}, /*index=5*/s32[]{:T...) while((s32[]{:T(128)}, f32[2,64,128]{2,1,0:T(8,128)S(1)}, ...), condition=%wide.region_11.13_spmd.clone.clone.clone, body=%wide.region_10.12_spmd.sunk.clone.clone.clone.sunk | while | flops 70322144 | bytes 2021583 | solution.py:162
  65.6 0.8 gather_fusion.5
  66.5 0.8 gather_fusion.4
  69.3 14.2 %fusion.249 = f32[2,64,128]{2,0,1:T(2,128)S(1)} fusion(f32[64,128]{1,0:T(8,128)S(1)} %bitcast.222, f32[64,128]{1,0:T(8,128)S(1)} %bitcast.228, f32[64,128]{1,0:T(8,128)S(1)} %bitcast.226, f32[64,128]{1,0:T(8,128)S(1)} %broadcast_add_fusion.19, f32[64,128]{1,0:T(8,128)S(1)} %bitcast.227, f32[64,128]{1,0:T(8,128)S(1)} %broadcast_add_fusion.20, ...), kind=kOutput, calls=%fused_computation.77.clone.1 | convolution fusion | flops 57671680 | bytes 409728 | tf_op jit(solution)/shard_map/while/body/gij,kgi->kgj/dot_general | solution.py:156
  83.8 18.1 %all_to_all.83 = f32[32,2,256]{2,1,0:T(2,128)S(1)} all-to-all(f32[32,2,256]{2,1,0:T(2,128)S(1)} %copy.39), channel_id=1, replica_groups=mesh['row_0'=8,'row_1'=2,'col_0'=8,'col_1'=4] {'col_0','col_1'}, dimensions={0} | all-to-all | bytes 131072 | tf_op jit(solution)/shard_map/all_to_all | solution.py:69
  102.3 14.1 %all_to_all.84 = f32[64,1,4]{2,1,0:T(1,128)S(1)} all-to-all(f32[64,1,4]{2,1,0:T(1,128)S(1)} %broadcast_in_dim.295), channel_id=1, replica_groups=mesh['row_0'=8,'row_1'=2,'col_0'=8,'col_1'=4] {'row_1','col_0','col_1'}, dimensions={0} | all-to-all | bytes 2048 | tf_op jit(solution)/shard_map/all_to_all | solution.py:29
  116.5 31.4 %all_to_all.85 = f32[8,1,4]{2,1,0:T(1,128)S(1)} all-to-all(f32[8,1,4]{2,1,0:T(1,128)S(1)} %broadcast_in_dim.296), channel_id=1, replica_groups=mesh['row_0'=8,'row_1'=2,'col_0'=8,'col_1'=4] {'row_0'}, dimensions={0} | all-to-all | bytes 256 | tf_op jit(solution)/shard_map/all_to_all | solution.py:29
  148.7 5.2 %all-to-all-start.5 = ((f32[16,2,256]{2,1,0:T(2,128)}), f32[16,2,256]{2,1,0:T(2,128)S(1)}, u32[]{:S(2)}, u32[]{:S(2)}) async-start(f32[16,2,256]{2,1,0:T(2,128)} %stack.10), calls=%async_computation.5 | async-start | bytes 65536 | tf_op jit(solution)/shard_map/all_to_all | solution.py:21
  153.9 7.5 %all-to-all-done.5 = f32[16,2,256]{2,1,0:T(2,128)S(1)} async-done(((f32[16,2,256]{2,1,0:T(2,128)}), f32[16,2,256]{2,1,0:T(2,128)S(1)}, u32[]{:S(2)}, u32[]{:S(2)}) %all-to-all-start.5) | async-done | bytes 32800 | tf_op jit(solution)/shard_map/all_to_all | solution.py:21
  161.4 21.0 %while.49 = (s32[]{:T(128)}, f32[2,64,128]{2,1,0:T(8,128)S(1)}, s32[]{:T(128)}, s32[2112]{0:T(1024)S(1)}, f32[2,32,128]{2,0,1:T(2,128)S(1)}, /*index=5*/s32[]{:T...) while((s32[]{:T(128)}, f32[2,64,128]{2,1,0:T(8,128)S(1)}, ...), condition=%wide.region_19.21_spmd.clone.clone.clone, body=%wide.region_18.20_spmd.sunk.clone.clone.clone.sunk | while | flops 70322144 | bytes 2021583 | solution.py:162
  164.2 0.8 gather_fusion.12
  168.0 14.2 %fusion.258 = f32[2,64,128]{2,0,1:T(2,128)S(1)} fusion(f32[64,128]{1,0:T(8,128)S(1)} %bitcast.223, f32[64,128]{1,0:T(8,128)S(1)} %bitcast.232, f32[64,128]{1,0:T(8,128)S(1)} %bitcast.230, f32[64,128]{1,0:T(8,128)S(1)} %broadcast_add_fusion.22, f32[64,128]{1,0:T(8,128)S(1)} %bitcast.231, f32[64,128]{1,0:T(8,128)S(1)} %broadcast_add_fusion.23, ...), kind=kOutput, calls=%fused_computation.161.clone.1 | convolution fusion | flops 57671680 | bytes 409728 | tf_op jit(solution)/shard_map/while/body/gij,kgi->kgj/dot_general | solution.py:156
  182.5 11.8 %all_to_all.86 = f32[32,2,256]{2,1,0:T(2,128)S(1)} all-to-all(f32[32,2,256]{2,1,0:T(2,128)S(1)} %copy.42), channel_id=1, replica_groups=mesh['row_0'=8,'row_1'=2,'col_0'=8,'col_1'=4] {'col_0','col_1'}, dimensions={0} | all-to-all | bytes 131072 | tf_op jit(solution)/shard_map/all_to_all | solution.py:69
  194.7 14.0 %all_to_all.87 = f32[64,1,4]{2,1,0:T(1,128)S(1)} all-to-all(f32[64,1,4]{2,1,0:T(1,128)S(1)} %broadcast_in_dim.297), channel_id=1, replica_groups=mesh['row_0'=8,'row_1'=2,'col_0'=8,'col_1'=4] {'row_1','col_0','col_1'}, dimensions={0} | all-to-all | bytes 2048 | tf_op jit(solution)/shard_map/all_to_all | solution.py:29
  208.8 29.1 %all_to_all.88 = f32[8,1,4]{2,1,0:T(1,128)S(1)} all-to-all(f32[8,1,4]{2,1,0:T(1,128)S(1)} %broadcast_in_dim.298), channel_id=1, replica_groups=mesh['row_0'=8,'row_1'=2,'col_0'=8,'col_1'=4] {'row_0'}, dimensions={0} | all-to-all | bytes 256 | tf_op jit(solution)/shard_map/all_to_all | solution.py:29
  238.7 5.2 %all-to-all-start.9 = ((f32[16,2,256]{2,1,0:T(2,128)}), f32[16,2,256]{2,1,0:T(2,128)S(1)}, u32[]{:S(2)}, u32[]{:S(2)}) async-start(f32[16,2,256]{2,1,0:T(2,128)} %stack.11), calls=%async_computation.9 | async-start | bytes 65536 | tf_op jit(solution)/shard_map/all_to_all | solution.py:21
  244.0 7.5 %all-to-all-done.9 = f32[16,2,256]{2,1,0:T(2,128)S(1)} async-done(((f32[16,2,256]{2,1,0:T(2,128)}), f32[16,2,256]{2,1,0:T(2,128)S(1)}, u32[]{:S(2)}, u32[]{:S(2)}) %all-to-all-start.9) | async-done | bytes 32800 | tf_op jit(solution)/shard_map/all_to_all | solution.py:21
  251.5 21.0 %while.50 = (s32[]{:T(128)}, f32[2,64,128]{2,1,0:T(8,128)S(1)}, s32[]{:T(128)}, s32[2112]{0:T(1024)S(1)}, f32[2,32,128]{2,0,1:T(2,128)S(1)}, /*index=5*/s32[]{:T...) while((s32[]{:T(128)}, f32[2,64,128]{2,1,0:T(8,128)S(1)}, ...), condition=%wide.region_26.28_spmd.clone.clone.clone, body=%wide.region_25.27_spmd.sunk.clone.clone.clone.sunk | while | flops 70322144 | bytes 2021583 | solution.py:162
  254.3 0.8 gather_fusion.19
  258.1 14.2 %fusion.267 = f32[2,64,128]{2,0,1:T(2,128)S(1)} fusion(f32[64,128]{1,0:T(8,128)S(1)} %bitcast.224, f32[64,128]{1,0:T(8,128)S(1)} %bitcast.236, f32[64,128]{1,0:T(8,128)S(1)} %bitcast.234, f32[64,128]{1,0:T(8,128)S(1)} %broadcast_add_fusion.25, f32[64,128]{1,0:T(8,128)S(1)} %bitcast.235, f32[64,128]{1,0:T(8,128)S(1)} %broadcast_add_fusion.26, ...), kind=kOutput, calls=%fused_computation.245.clone.1 | convolution fusion | flops 57671680 | bytes 409728 | tf_op jit(solution)/shard_map/while/body/gij,kgi->kgj/dot_general | solution.py:156
  272.6 11.8 %all_to_all.89 = f32[32,2,256]{2,1,0:T(2,128)S(1)} all-to-all(f32[32,2,256]{2,1,0:T(2,128)S(1)} %copy.45), channel_id=1, replica_groups=mesh['row_0'=8,'row_1'=2,'col_0'=8,'col_1'=4] {'col_0','col_1'}, dimensions={0} | all-to-all | bytes 131072 | tf_op jit(solution)/shard_map/all_to_all | solution.py:69
  284.7 14.0 %all_to_all.90 = f32[64,1,4]{2,1,0:T(1,128)S(1)} all-to-all(f32[64,1,4]{2,1,0:T(1,128)S(1)} %broadcast_in_dim.299), channel_id=1, replica_groups=mesh['row_0'=8,'row_1'=2,'col_0'=8,'col_1'=4] {'row_1','col_0','col_1'}, dimensions={0} | all-to-all | bytes 2048 | tf_op jit(solution)/shard_map/all_to_all | solution.py:29
  298.9 29.1 %all_to_all.91 = f32[8,1,4]{2,1,0:T(1,128)S(1)} all-to-all(f32[8,1,4]{2,1,0:T(1,128)S(1)} %broadcast_in_dim.300), channel_id=1, replica_groups=mesh['row_0'=8,'row_1'=2,'col_0'=8,'col_1'=4] {'row_0'}, dimensions={0} | all-to-all | bytes 256 | tf_op jit(solution)/shard_map/all_to_all | solution.py:29
  328.3 14.5 %all_to_all.92 = f32[64,1,2]{2,1,0:T(1,128)S(1)} all-to-all(f32[64,1,2]{2,1,0:T(1,128)S(1)} %broadcast_in_dim.301), channel_id=1, replica_groups=mesh['row_0'=8,'row_1'=2,'col_0'=8,'col_1'=4] {'row_1','col_0','col_1'}, dimensions={0} | all-to-all | bytes 1024 | tf_op jit(solution)/shard_map/all_to_all | solution.py:29
  342.9 8.9 %all_to_all.93 = f32[8,1,2]{2,1,0:T(1,128)S(1)} all-to-all(f32[8,1,2]{2,1,0:T(1,128)S(1)} %broadcast_in_dim.302), channel_id=1, replica_groups=mesh['row_0'=8,'row_1'=2,'col_0'=8,'col_1'=4] {'row_0'}, dimensions={0} | all-to-all | bytes 128 | tf_op jit(solution)/shard_map/all_to_all | solution.py:29
  (156 shorter events, 26.6 us)
Async XLA Ops:
  1.4 31.4 %all-to-all-start = ((f32[16,2,256]{2,1,0:T(2,128)}), f32[16,2,256]{2,1,0:T(2,128)S(1)}, u32[]{:S(2)}, u32[]{:S(2)}) async-start(f32[16,2,256]{2,1,0:T(2,128)} %stack.9), calls=%async_computation | async-start | bytes 65536 | tf_op jit(solution)/shard_map/all_to_all | solution.py:21
  13.0 19.9 %copy-start.3 = (f32[3,256]{1,0:T(4,128)S(1)}, f32[3,256]{1,0:T(4,128)}, u32[]{:S(2)}) copy-start(f32[3,256]{1,0:T(4,128)} %param.16) | copy-start | bytes 9220
  14.8 47.8 %copy-start = (s32[3]{0:T(128)S(1)}, s32[3]{0:T(128)}, u32[]{:S(2)}) copy-start(s32[3]{0:T(128)} %constant.962) | copy-start | bytes 40
  14.8 47.8 %copy-start.1 = (s32[3]{0:T(128)S(1)}, s32[3]{0:T(128)}, u32[]{:S(2)}) copy-start(s32[3]{0:T(128)} %constant.963) | copy-start | bytes 40
  14.8 47.8 %copy-start.2 = (s32[3]{0:T(128)S(1)}, s32[3]{0:T(128)}, u32[]{:S(2)}) copy-start(s32[3]{0:T(128)} %constant.964) | copy-start | bytes 40
  33.5 29.1 %all-to-all-start.1 = ((f32[32,4,256]{2,1,0:T(4,128)}), f32[32,4,256]{2,1,0:T(4,128)S(1)}, u32[]{:S(2)}, u32[]{:S(2)}) async-start(f32[32,4,256]{2,1,0:T(4,128)} %broadcast_in_dim.293), calls=%async_computation.1 | async-start | bytes 262144 | tf_op jit(solution)/shard_map/all_to_all | solution.py:29
  148.7 12.7 %all-to-all-start.5 = ((f32[16,2,256]{2,1,0:T(2,128)}), f32[16,2,256]{2,1,0:T(2,128)S(1)}, u32[]{:S(2)}, u32[]{:S(2)}) async-start(f32[16,2,256]{2,1,0:T(2,128)} %stack.10), calls=%async_computation.5 | async-start | bytes 65536 | tf_op jit(solution)/shard_map/all_to_all | solution.py:21
  238.7 12.7 %all-to-all-start.9 = ((f32[16,2,256]{2,1,0:T(2,128)}), f32[16,2,256]{2,1,0:T(2,128)S(1)}, u32[]{:S(2)}, u32[]{:S(2)}) async-start(f32[16,2,256]{2,1,0:T(2,128)} %stack.11), calls=%async_computation.9 | async-start | bytes 65536 | tf_op jit(solution)/shard_map/all_to_all | solution.py:21
